TPU v7x, 32 devices: a whole 2x2x4 slice. The times are simulated.
32 devices in a mesh: fsdp: 8 (over z, core), cols: 4 (over y, x).
Axes of the slice: x: 2, y: 2, z: 4, core: 2. Of those that a mesh axis runs over, the one named last changes fastest.
Arguments:
- weight_query: bfloat16 [5120, 5120], P('fsdp', 'cols'), may hold values from -0.078125 to 0.078125
- low_query: bfloat16 [5120, 32], P('fsdp'), may hold values from -0.078125 to 0.078125
- high_query: bfloat16 [32, 5120], P(None, 'cols'), may hold values from -1 to 1
- weight_key: bfloat16 [5120, 5120], P('fsdp', 'cols'), may hold values from -0.078125 to 0.078125
- low_key: bfloat16 [5120, 32], P('fsdp'), may hold values from -0.078125 to 0.078125
- high_key: bfloat16 [32, 5120], P(None, 'cols'), may hold values from -1 to 1
- weight_value: bfloat16 [5120, 5120], P('fsdp', 'cols'), may hold values from -0.078125 to 0.078125
- low_value: bfloat16 [5120, 32], P('fsdp'), may hold values from -0.078125 to 0.078125
- high_value: bfloat16 [32, 5120], P(None, 'cols'), may hold values from -1 to 1
- weight_mixed: bfloat16 [5120, 5120], P('cols', 'fsdp'), may hold values from -0.078125 to 0.078125
- low_mixed: bfloat16 [5120, 32], P('cols'), may hold values from -0.078125 to 0.078125
- high_mixed: bfloat16 [32, 5120], P(None, 'fsdp'), may hold values from -1 to 1
- norm_train: float32 [5120], P(('fsdp', 'cols')), may hold values from 0.25 to 1.75
- norm_step: float32 [5120], P(('fsdp', 'cols')), may hold values from -0.3 to 0.3
Outputs:
- ready_query: bfloat16 [5120, 5120], P(None, 'cols')
- ready_key: bfloat16 [5120, 5120], P(None, 'cols')
- ready_value: bfloat16 [5120, 5120], P(None, 'cols')
- ready_mixed: bfloat16 [5120, 5120], P('cols')
- serve_norm: bfloat16 [5120], replicated
All inputs are finite; a program needn't handle non-finite values.
Results may differ from a plain program's by a relative error of at most 0.001.
Values may be sent and summed in bfloat16 or wider, within the bound.
A program may use at most 192 MiB of HBM per device.

v0:
```python
import jax
import jax.numpy as jnp
from jax import lax
from jax.sharding import PartitionSpec as P

mix_rate = 2.0


def per_device(
    weight_query,
    low_query,
    high_query,
    weight_key,
    low_key,
    high_key,
    weight_value,
    low_value,
    high_value,
    weight_mixed,
    low_mixed,
    high_mixed,
    norm_train,
    norm_step,
):
    (
        moved_query,
        moved_key,
        moved_value,
        moved_mixed,
        factor_query,
        factor_key,
        factor_value,
        factor_mixed,
    ) = (
        lax.all_gather(weight_query, "fsdp", axis=0, tiled=True),
        lax.all_gather(weight_key, "fsdp", axis=0, tiled=True),
        lax.all_gather(weight_value, "fsdp", axis=0, tiled=True),
        lax.all_gather(weight_mixed, "fsdp", axis=1, tiled=True),
        lax.all_gather(low_query, "fsdp", axis=0, tiled=True),
        lax.all_gather(low_key, "fsdp", axis=0, tiled=True),
        lax.all_gather(low_value, "fsdp", axis=0, tiled=True),
        lax.all_gather(high_mixed, "fsdp", axis=1, tiled=True),
    )
    latest_query = moved_query.astype(jnp.float32) + mix_rate * jnp.dot(
        factor_query, high_query, preferred_element_type=jnp.float32
    )
    ready_query = latest_query.astype(jnp.bfloat16)
    latest_key = moved_key.astype(jnp.float32) + mix_rate * jnp.dot(
        factor_key, high_key, preferred_element_type=jnp.float32
    )
    ready_key = latest_key.astype(jnp.bfloat16)
    latest_value = moved_value.astype(jnp.float32) + mix_rate * jnp.dot(
        factor_value, high_value, preferred_element_type=jnp.float32
    )
    ready_value = latest_value.astype(jnp.bfloat16)
    latest_mixed = moved_mixed.astype(jnp.float32) + mix_rate * jnp.dot(
        low_mixed, factor_mixed, preferred_element_type=jnp.float32
    )
    ready_mixed = latest_mixed.astype(jnp.bfloat16)
    serve_norm = lax.all_gather(
        (norm_train + norm_step).astype(jnp.bfloat16), ("fsdp", "cols"), axis=0, tiled=True
    )
    return (ready_query, ready_key, ready_value, ready_mixed, serve_norm)


def solution(mesh):
    in_specs = (
        P("fsdp", "cols"),
        P("fsdp", None),
        P(None, "cols"),
        P("fsdp", "cols"),
        P("fsdp", None),
        P(None, "cols"),
        P("fsdp", "cols"),
        P("fsdp", None),
        P(None, "cols"),
        P("cols", "fsdp"),
        P("cols", None),
        P(None, "fsdp"),
        P(("fsdp", "cols")),
        P(("fsdp", "cols")),
    )
    out_specs = (P(None, "cols"), P(None, "cols"), P(None, "cols"), P("cols", None), P())
    return jax.shard_map(
        per_device, mesh=mesh, in_specs=in_specs, out_specs=out_specs, check_vma=False
    )
```

profile of v0, /device:TPU:0, one launch (start us, length us, event | category | flops | bytes accessed | tf_op | source)
XLA Modules:
  0.0 523.4 jit_solution(16117009609130289088)
XLA Ops:
  7.2 0.0 copy-start
  7.2 0.0 all-gather.11.cloned.1.call-start
  7.2 0.7 all-gather.11.cloned.1.call-update
  7.9 0.0 all-gather.9.cloned.1.call-start
  8.0 0.7 all-gather.9.cloned.1.call-update
  8.7 0.0 all-gather.7.cloned.1.call-start
  8.7 0.7 all-gather.7.cloned.1.call-update
  9.4 0.0 all-gather.5.cloned.1.call-start
  9.4 0.5 all-gather.5.cloned.1.call-update
  10.0 0.7 add_convert_fusion.4
  10.7 0.2 dynamic-update-slice
  10.9 47.5 %all-reduce = bf16[5120]{0:T(1024)(128)(2,1)} all-reduce(bf16[5120]{0:T(1024)(128)(2,1)S(1)} %dynamic-update-slice), channel_id=1, replica_groups=mesh['fsdp'=8,'cols'=4] {'fsdp','cols'}, use_global_device_ids=true, to_apply=%add | all-reduce | flops 5120 | bytes 20480
  58.4 19.3 %all_gather.34 = bf16[32,5120]{1,0:T(8,128)(2,1)S(1)} all-gather(bf16[32,640]{1,0:T(8,128)(2,1)} %param.25), channel_id=1, replica_groups=mesh['fsdp'=8,'cols'=4] {'fsdp'}, dimensions={1}, use_global_device_ids=true | all-gather | bytes 368640 | tf_op jit(solution)/shard_map/all_gather | solution.py:42
  77.7 18.9 %all_gather.32 = bf16[5120,32]{0,1:T(8,128)(2,1)S(1)} all-gather(bf16[640,32]{0,1:T(8,128)(2,1)} %param.21), channel_id=1, replica_groups=mesh['fsdp'=8,'cols'=4] {'fsdp'}, dimensions={0}, use_global_device_ids=true | all-gather | bytes 368640 | tf_op jit(solution)/shard_map/all_gather | solution.py:41
  96.6 22.4 %all_gather.30 = bf16[5120,32]{0,1:T(8,128)(2,1)S(1)} all-gather(bf16[640,32]{0,1:T(8,128)(2,1)} %param.18), channel_id=1, replica_groups=mesh['fsdp'=8,'cols'=4] {'fsdp'}, dimensions={0}, use_global_device_ids=true | all-gather | bytes 368640 | tf_op jit(solution)/shard_map/all_gather | solution.py:40
  119.0 18.5 %all_gather.28 = bf16[5120,32]{0,1:T(8,128)(2,1)S(1)} all-gather(bf16[640,32]{0,1:T(8,128)(2,1)} %param.15), channel_id=1, replica_groups=mesh['fsdp'=8,'cols'=4] {'fsdp'}, dimensions={0}, use_global_device_ids=true | all-gather | bytes 368640 | tf_op jit(solution)/shard_map/all_gather | solution.py:39
  137.4 0.0 copy-start.2
  137.4 7.2 %all-gather.11.cloned.1.call-done = bf16[1280,5120]{1,0:T(8,128)(2,1)} async-done(((bf16[1280,640]{1,0:T(8,128)(2,1)}), bf16[1280,5120]{1,0:T(8,128)(2,1)}) %all-gather.11.cloned.1.call-update) | async-done | bytes 13107216 | tf_op jit(solution)/shard_map/all_gather | solution.py:38
  144.6 0.0 copy-done
  144.6 10.6 %add_convert_fusion = bf16[1280,5120]{1,0:T(8,128)(2,1)} fusion(bf16[1280,5120]{1,0:T(8,128)(2,1)} %all-gather.11.cloned.1.call-done, bf16[1280,32]{0,1:T(8,128)(2,1)S(1)} %copy-done, bf16[32,5120]{1,0:T(8,128)(2,1)S(1)} %all_gather.34), kind=kOutput, calls=%fused_computation | convolution fusion | flops 445644800 | bytes 26624000 | tf_op jit(solution)/shard_map/dot_general | solution.py:56
  155.2 0.0 copy-start.3
  155.2 110.3 %all-gather.9.cloned.1.call-done = bf16[5120,1280]{1,0:T(8,128)(2,1)} async-done(((bf16[640,1280]{1,0:T(8,128)(2,1)}), bf16[5120,1280]{1,0:T(8,128)(2,1)}) %all-gather.9.cloned.1.call-update) | async-done | bytes 13107216 | tf_op jit(solution)/shard_map/all_gather | solution.py:37
  265.5 0.0 copy-done.2
  265.5 10.7 %add_convert_fusion.1 = bf16[5120,1280]{1,0:T(8,128)(2,1)} fusion(bf16[5120,1280]{1,0:T(8,128)(2,1)} %all-gather.9.cloned.1.call-done, bf16[5120,32]{0,1:T(8,128)(2,1)S(1)} %all_gather.32, bf16[32,1280]{1,0:T(8,128)(2,1)S(1)} %copy-done.2), kind=kOutput, calls=%fused_computation.1 | convolution fusion | flops 445644800 | bytes 26624000 | tf_op jit(solution)/shard_map/dot_general | solution.py:52
  276.2 0.0 copy-start.4
  276.2 110.2 %all-gather.7.cloned.1.call-done = bf16[5120,1280]{1,0:T(8,128)(2,1)} async-done(((bf16[640,1280]{1,0:T(8,128)(2,1)}), bf16[5120,1280]{1,0:T(8,128)(2,1)}) %all-gather.7.cloned.1.call-update) | async-done | bytes 13107216 | tf_op jit(solution)/shard_map/all_gather | solution.py:36
  386.4 0.0 copy-done.3
  386.4 0.0 copy-start.1
  386.4 10.9 %add_convert_fusion.2 = bf16[5120,1280]{1,0:T(8,128)(2,1)} fusion(bf16[5120,1280]{1,0:T(8,128)(2,1)} %all-gather.7.cloned.1.call-done, bf16[5120,32]{0,1:T(8,128)(2,1)S(1)} %all_gather.30, bf16[32,1280]{1,0:T(8,128)(2,1)S(1)} %copy-done.3), kind=kOutput, calls=%fused_computation.2 | convolution fusion | flops 445644800 | bytes 26624000 | tf_op jit(solution)/shard_map/dot_general | solution.py:48
  397.3 109.8 %all-gather.5.cloned.1.call-done = bf16[5120,1280]{1,0:T(8,128)(2,1)} async-done(((bf16[640,1280]{1,0:T(8,128)(2,1)}), bf16[5120,1280]{1,0:T(8,128)(2,1)}) %all-gather.5.cloned.1.call-update) | async-done | bytes 13107216 | tf_op jit(solution)/shard_map/all_gather | solution.py:35
  507.1 0.0 copy-done.4
  507.1 9.7 %add_convert_fusion.3 = bf16[5120,1280]{1,0:T(8,128)(2,1)} fusion(bf16[5120,1280]{1,0:T(8,128)(2,1)} %all-gather.5.cloned.1.call-done, bf16[5120,32]{0,1:T(8,128)(2,1)S(1)} %all_gather.28, bf16[32,1280]{1,0:T(8,128)(2,1)S(1)} %copy-done.4), kind=kOutput, calls=%fused_computation.3 | convolution fusion | flops 445644800 | bytes 26624000 | tf_op jit(solution)/shard_map/dot_general | solution.py:44
  516.8 0.0 copy-done.1
  (1 shorter events, 0.0 us)
Async XLA Ops:
  7.2 137.4 %copy-start = (bf16[1280,32]{0,1:T(8,128)(2,1)S(1)}, bf16[1280,32]{0,1:T(8,128)(2,1)}, u32[]{:S(2)}) copy-start(bf16[1280,32]{0,1:T(8,128)(2,1)} %param.24) | copy-start | bytes 245764
  7.2 137.4 %all-gather.11.cloned.1.call-start = ((), (), s32[]{:S(2)}) async-start(), calls=%async_computation.3 | async-start | bytes 14745600 | tf_op jit(solution)/shard_map/all_gather | solution.py:38
  7.9 257.6 %all-gather.9.cloned.1.call-start = ((), (), s32[]{:S(2)}) async-start(), calls=%async_computation.2 | async-start | bytes 14745600 | tf_op jit(solution)/shard_map/all_gather | solution.py:37
  8.7 377.7 %all-gather.7.cloned.1.call-start = ((), (), s32[]{:S(2)}) async-start(), calls=%async_computation.1 | async-start | bytes 14745600 | tf_op jit(solution)/shard_map/all_gather | solution.py:36
  9.4 497.7 %all-gather.5.cloned.1.call-start = ((), (), s32[]{:S(2)}) async-start(), calls=%async_computation | async-start | bytes 14745600 | tf_op jit(solution)/shard_map/all_gather | solution.py:35
  137.4 128.1 %copy-start.2 = (bf16[32,1280]{1,0:T(8,128)(2,1)S(1)}, bf16[32,1280]{1,0:T(8,128)(2,1)}, u32[]{:S(2)}) copy-start(bf16[32,1280]{1,0:T(8,128)(2,1)} %param.22) | copy-start | bytes 245764
  155.2 231.2 %copy-start.3 = (bf16[32,1280]{1,0:T(8,128)(2,1)S(1)}, bf16[32,1280]{1,0:T(8,128)(2,1)}, u32[]{:S(2)}) copy-start(bf16[32,1280]{1,0:T(8,128)(2,1)} %param.19) | copy-start | bytes 245764
  276.2 230.9 %copy-start.4 = (bf16[32,1280]{1,0:T(8,128)(2,1)S(1)}, bf16[32,1280]{1,0:T(8,128)(2,1)}, u32[]{:S(2)}) copy-start(bf16[32,1280]{1,0:T(8,128)(2,1)} %param.16) | copy-start | bytes 245764
  386.4 130.5 %copy-start.1 = (bf16[1280,32]{0,1:T(8,128)(2,1)S(1)}, bf16[1280,32]{0,1:T(8,128)(2,1)}, u32[]{:S(2)}) copy-start(bf16[1280,32]{0,1:T(8,128)(2,1)} %param.24) | copy-start | bytes 245764
Sparse Core Ops, SparseCore 0:
  9.6 134.9 all-gather.10
  146.2 119.2 all-gather.8
  267.2 119.1 all-gather.6
  387.9 119.1 all-gather.4
where the time goes:
time: 524 us; the launch traced here: 523 us
  waiting for transfers between devices  340 us (65%)
  blocking collectives  127 us (24%)
  matrix products  41.9 us (8%)
  between operations  13.8 us (3%)
    all_gather x1, waiting for transfers between devices, per_device(): lax.all_gather(weight_value, 'fsdp', axis=0, tiled=True)  110 us
    all_gather x1, waiting for transfers between devices, per_device(): lax.all_gather(weight_key, 'fsdp', axis=0, tiled=True)  110 us
    all_gather x1, waiting for transfers between devices, per_device(): lax.all_gather(weight_query, 'fsdp', axis=0, tiled=True)  110 us
    unnamed x1, blocking collectives  47.5 us
    all_gather x1, blocking collectives, per_device(): lax.all_gather(low_key, 'fsdp', axis=0, tiled=True)  22.4 us
    all_gather x1, blocking collectives, per_device(): lax.all_gather(high_mixed, 'fsdp', axis=1, tiled=True)  19.3 us
    all_gather x1, blocking collectives, per_device(): lax.all_gather(low_value, 'fsdp', axis=0, tiled=True)  18.9 us
    all_gather x1, blocking collectives, per_device(): lax.all_gather(low_query, 'fsdp', axis=0, tiled=True)  18.5 us
  transfers between devices with their start and end apart: 4, of which 4 were waited for; matrix products, arithmetic and copies ran while one was open for 6% of the time, Pallas kernels for 0%

commit v1 on v0

v1 whole, which is shorter than its diff:
```python
import functools

import jax
import jax.numpy as jnp
from jax import lax
from jax.experimental import pallas as pl
from jax.experimental.pallas import tpu as pltpu
from jax.sharding import PartitionSpec as P

mix_rate = 2.0
MESH = pl.DeviceIdType.MESH
ROW_TILE = 128
BY_ROWS = (True, True, False, True)
LAST = len(BY_ROWS) - 1


def block_of(ref, by_rows, index, extent):
    if len(ref.shape) == 3:
        return ref.at[index]
    if by_rows:
        return ref.at[pl.ds(pl.multiple_of(index * extent, extent), extent), :]
    return ref.at[:, pl.ds(pl.multiple_of(index * extent, extent), extent)]


def gather_kernel(spots, has_tail, *refs):
    weights, lows, highs = refs[0:4], refs[4:8], refs[8:12]
    outs = refs[12:16]
    raw, ready = refs[16:20], refs[20:24]
    in_sem, own_sem, send_r, recv_r, send_l, recv_l, send_d, recv_d = refs[24:]
    me = lax.axis_index("fsdp")
    spot, core = lax.div(me, 2), lax.rem(me, 2)
    last = spots - 1
    number = len(BY_ROWS)

    loads = [pltpu.make_async_copy(weights[w], raw[w], in_sem.at[w]) for w in range(number)]
    for load in loads:
        load.start()

    barrier = pltpu.get_barrier_semaphore()

    def greet(target):
        pl.semaphore_signal(barrier, inc=1, device_id={"fsdp": target}, device_id_type=MESH)

    greet(2 * spot + 1 - core)

    @pl.when(spot > 0)
    def _():
        greet(me - 2)

    @pl.when(spot < last)
    def _():
        greet(me + 2)

    peers = 1 + (spot > 0).astype(jnp.int32) + (spot < last).astype(jnp.int32)
    pl.semaphore_wait(barrier, peers)

    def block(w, origin, side):
        extent = weights[w].shape[0 if BY_ROWS[w] else 1]
        return block_of(outs[w], BY_ROWS[w], 2 * origin + side, extent)

    def remote(w, origin, side, target, send, recv):
        piece = block(w, origin, side)
        return pltpu.make_async_remote_copy(
            src_ref=piece,
            dst_ref=piece,
            send_sem=send,
            recv_sem=recv,
            device_id={"fsdp": target},
            device_id_type=MESH,
        )

    def rightward(w, step, origin):
        return remote(w, origin, core, me + 2, send_r.at[w, step], recv_r.at[w, step])

    def leftward(w, step, origin):
        return remote(w, origin, core, me - 2, send_l.at[w, step], recv_l.at[w, step])

    def across(w, slot, origin, side):
        return remote(w, origin, side, 2 * spot + 1 - core, send_d.at[w, slot], recv_d.at[w, slot])

    def travels(w, step):
        return step <= last and not (has_tail and w == LAST and step == last)

    for w in range(number):
        loads[w].wait()
        rows = weights[w].shape[0]
        height = rows if rows % ROW_TILE else ROW_TILE

        def merge(tile, carry, w=w, height=height):
            start = pl.multiple_of(tile * height, height) if height < weights[w].shape[0] else 0
            product = lax.dot_general(
                lows[w][:, pl.ds(start, height)],
                highs[w][...],
                (((0,), (0,)), ((), ())),
                preferred_element_type=jnp.float32,
            )
            base = raw[w][pl.ds(start, height), :].astype(jnp.float32)
            ready[w][pl.ds(start, height), :] = (base + mix_rate * product).astype(jnp.bfloat16)
            return carry

        lax.fori_loop(0, rows // height, merge, 0)
        keep = pltpu.make_async_copy(ready[w], block(w, spot, core), own_sem.at[w])
        keep.start()
        keep.wait()
        if travels(w, 1):

            @pl.when(spot < last)
            def _():
                rightward(w, 1, spot).start()

            @pl.when(spot > 0)
            def _():
                leftward(w, 1, spot).start()

        across(w, 0, spot, core).start()

    for step in range(1, spots):
        for w in range(number):
            if not travels(w, step):
                continue

            @pl.when(spot - step >= 0)
            def _():
                rightward(w, step, spot - step).wait_recv()
                if travels(w, step + 1):

                    @pl.when(spot < last)
                    def _():
                        rightward(w, step + 1, spot - step).start()

                across(w, step, spot - step, core).start()

            @pl.when(spot + step <= last)
            def _():
                leftward(w, step, spot + step).wait_recv()
                if travels(w, step + 1):

                    @pl.when(spot > 0)
                    def _():
                        leftward(w, step + 1, spot + step).start()

                across(w, last + step, spot + step, core).start()

    for w in range(number):
        across(w, 0, spot, core).wait_send()
        across(w, 0, spot, 1 - core).wait_recv()
        for step in range(1, spots):
            if not travels(w, step):
                continue

            @pl.when((spot < last) & (spot - step + 1 >= 0))
            def _():
                rightward(w, step, spot - step + 1).wait_send()

            @pl.when((spot > 0) & (spot + step - 1 <= last))
            def _():
                leftward(w, step, spot + step - 1).wait_send()

            @pl.when(spot - step >= 0)
            def _():
                across(w, step, spot - step, core).wait_send()
                across(w, step, spot - step, 1 - core).wait_recv()

            @pl.when(spot + step <= last)
            def _():
                across(w, last + step, spot + step, core).wait_send()
                across(w, last + step, spot + step, 1 - core).wait_recv()


def copy_kernel(*refs):
    number = len(refs) // 2
    for w in range(number):
        refs[number + w][...] = refs[w][...]


def patch_kernel(spots, got_ref, other_ref, base_ref, out_ref, got, other, sem):
    me = lax.axis_index("fsdp")
    spot, core = lax.div(me, 2), lax.rem(me, 2)
    extent = got_ref.shape[0]

    @pl.when((spot == 0) | (spot == spots - 1))
    def _():
        origin = spots - 1 - spot
        loads = [
            pltpu.make_async_copy(got_ref, got, sem.at[0]),
            pltpu.make_async_copy(other_ref, other, sem.at[1]),
        ]
        stores = [
            pltpu.make_async_copy(
                got, block_of(out_ref, True, 2 * origin + core, extent), sem.at[2]
            ),
            pltpu.make_async_copy(
                other, block_of(out_ref, True, 2 * origin + 1 - core, extent), sem.at[3]
            ),
        ]
        for load in loads:
            load.start()
        for load, store in zip(loads, stores):
            load.wait()
            store.start()
        for store in stores:
            store.wait()


def per_device(
    fsdp,
    weight_query,
    low_query,
    high_query,
    weight_key,
    low_key,
    high_key,
    weight_value,
    low_value,
    high_value,
    weight_mixed,
    low_mixed,
    high_mixed,
    norm_train,
    norm_step,
):
    spots = fsdp // 2
    has_tail = spots >= 4
    weights = (weight_query, weight_key, weight_mixed, weight_value)
    lows = (low_query.T, low_key.T, low_mixed.T, low_value.T)
    highs = (high_query, high_key, high_mixed, high_value)
    number = len(weights)
    whole = tuple(
        jax.ShapeDtypeStruct(
            (x.shape[0] * fsdp, x.shape[1]) if by_rows else (x.shape[0], x.shape[1] * fsdp),
            jnp.bfloat16,
        )
        for x, by_rows in zip(weights, BY_ROWS)
    )
    stacked = tuple(not by_rows and x.shape[1] % 128 != 0 for x, by_rows in zip(weights, BY_ROWS))
    landing = tuple(
        jax.ShapeDtypeStruct((fsdp, *x.shape), jnp.bfloat16) if apart else full
        for x, full, apart in zip(weights, whole, stacked)
    )
    anywhere = pl.BlockSpec(memory_space=pl.ANY)
    inside = pl.BlockSpec(memory_space=pltpu.VMEM)
    dma = pltpu.SemaphoreType.DMA
    gathered = pl.pallas_call(
        functools.partial(gather_kernel, spots, has_tail),
        out_shape=landing,
        in_specs=[anywhere] * number + [inside] * (2 * number),
        out_specs=[anywhere] * number,
        scratch_shapes=[pltpu.VMEM(x.shape, jnp.bfloat16) for x in weights] * 2
        + [dma((number,))] * 2
        + [dma((number, spots))] * 4
        + [dma((number, 2 * spots - 1))] * 2,
        compiler_params=pltpu.CompilerParams(
            collective_id=0, has_side_effects=True, vmem_limit_bytes=60 * 2**20
        ),
        name="gather",
    )(*weights, *lows, *highs)

    me = lax.axis_index("fsdp")
    spot, core = me // 2, me % 2
    extent = weight_value.shape[0]
    if has_tail:
        origin = jnp.where(spot == 1, spots - 1, 0)
        edge = lax.dynamic_slice_in_dim(gathered[LAST], (2 * origin + core) * extent, extent, 0)
        ends = [(2 * (spots - 2) + side, 2 * (spots - 1) + side) for side in range(2)]
        ends += [(2 + side, side) for side in range(2)]
        got = lax.ppermute(edge, "fsdp", ends)
        swap = [(i, i ^ 1) for i in (0, 1, fsdp - 2, fsdp - 1)]

    settled = [w for w in range(number) if not stacked[w]]
    specs = [
        pl.BlockSpec(weights[w].shape, (lambda i: (i, 0)) if BY_ROWS[w] else (lambda i: (0, i)))
        for w in settled
    ]
    moved = 2 * sum(2 * x.shape[0] * x.shape[1] for x in whole)
    ready = pl.pallas_call(
        copy_kernel,
        grid=(fsdp,),
        out_shape=[whole[w] for w in settled],
        in_specs=specs,
        out_specs=specs,
        compiler_params=pltpu.CompilerParams(vmem_limit_bytes=48 * 2**20),
        cost_estimate=pl.CostEstimate(flops=0, bytes_accessed=moved, transcendentals=0),
        name="settle",
    )(*[gathered[w] for w in settled])
    finished = dict(zip(settled, ready))
    for w in range(number):
        if stacked[w]:
            finished[w] = gathered[w].transpose(1, 0, 2).reshape(whole[w].shape)
    ready_query, ready_key, ready_mixed, ready_value = (finished[w] for w in range(number))
    if has_tail:
        got, ready_value = lax.optimization_barrier((got, ready_value))
        other = lax.ppermute(got, "fsdp", swap)
        ready_value = pl.pallas_call(
            functools.partial(patch_kernel, spots),
            out_shape=whole[LAST],
            in_specs=[anywhere] * 3,
            out_specs=anywhere,
            scratch_shapes=[pltpu.VMEM(weight_value.shape, jnp.bfloat16)] * 2 + [dma((4,))],
            input_output_aliases={2: 0},
            compiler_params=pltpu.CompilerParams(vmem_limit_bytes=16 * 2**20),
            name="patch",
        )(got, other, ready_value)

    serve_norm = lax.all_gather(
        (norm_train + norm_step).astype(jnp.bfloat16), ("fsdp", "cols"), axis=0, tiled=True
    )
    return (ready_query, ready_key, ready_value, ready_mixed, serve_norm)


def solution(mesh):
    in_specs = (
        P("fsdp", "cols"),
        P("fsdp", None),
        P(None, "cols"),
        P("fsdp", "cols"),
        P("fsdp", None),
        P(None, "cols"),
        P("fsdp", "cols"),
        P("fsdp", None),
        P(None, "cols"),
        P("cols", "fsdp"),
        P("cols", None),
        P(None, "fsdp"),
        P(("fsdp", "cols")),
        P(("fsdp", "cols")),
    )
    out_specs = (P(None, "cols"), P(None, "cols"), P(None, "cols"), P("cols", None), P())
    return jax.shard_map(
        functools.partial(per_device, mesh.shape["fsdp"]),
        mesh=mesh,
        in_specs=in_specs,
        out_specs=out_specs,
        check_vma=False,
    )
```

time: 524 us -> 486 us (0.927)
  Pallas kernels: 0 us -> 436 us
  waiting for transfers between devices: 340 us -> 5.1 us
  blocking collectives: 127 us -> 38.9 us
  matrix products: 41.9 us -> 0 us
  between operations: 13.8 us -> 0.75 us
    pallas_call x0 -> x3, Pallas kernels: none -> 436 us  [the longest x1 400 us: per_device(): pl.pallas_call(functools.partial(gather_kernel, spots, has_tail), out_sha...]
    all_gather x4 -> x0, waiting for transfers between devices: 337 us -> none  [the longest x1 110 us: per_device(): lax.all_gather(weight_value, 'fsdp', axis=0, tiled=True)]
    all_gather x4 -> x0, blocking collectives: 79 us -> none  [the longest x1 22.4 us: per_device(): lax.all_gather(low_key, 'fsdp', axis=0, tiled=True)]
    dot_general x4 -> x0, matrix products: 41.9 us -> none  [the longest x1 10.9 us: per_device(): jnp.dot(factor_key, high_key, preferred_element_type=jnp.float32)]
    unnamed x1, blocking collectives: 47.5 us -> 38.9 us
  transfers between devices with their start and end apart: 4 -> 2, of which waited for: 4 -> 1; matrix products, arithmetic and copies ran while one was open for 6% -> 0% of each run, Pallas kernels for 0% -> 7%
where the time goes in v1:
time: 486 us
  Pallas kernels  436 us (90%)
  blocking collectives  38.9 us (8%)
  waiting for transfers between devices  5.1 us (1%)
    pallas_call x1, Pallas kernels, per_device(): pl.pallas_call(functools.partial(gather_kernel, spots, has_tail), out_sha...  400 us
    unnamed x1, blocking collectives  38.9 us
    pallas_call x1, Pallas kernels, per_device(): pl.pallas_call(copy_kernel, grid=(fsdp,), out_shape=[whole[w] for w in se...  33.5 us
  transfers between devices with their start and end apart: 2, of which 1 were waited for; matrix products, arithmetic and copies ran while one was open for 0% of the time, Pallas kernels for 7%

profile of v1, /device:TPU:0, one launch (start us, length us, event | category | flops | bytes accessed | tf_op | source)
XLA Modules:
  0.0 485.5 jit_solution(2981299407965753718)
XLA Ops:
  0.7 400.1 %gather.1 = (bf16[5120,1280]{1,0:T(8,128)(2,1)}, bf16[5120,1280]{1,0:T(8,128)(2,1)}, bf16[1280,5120]{1,0:T(8,128)(2,1)}, bf16[5120,1280]{1,0:T(8,128)(2,1)}) custom-call(bf16[640,1280]{1,0:T(8,128)(2,1)} %refs_0_.1, bf16[640,1280]{1,0:T(8,128)(2,1)} %refs_1_.1, bf16[1280,640]{1,0:T(8,128)(2,1)} %refs_2_.1, bf16[640,1280]{1,0:T(8,128)(2,1)} %refs_3_.1, ...), custom_call_target="tpu_custom_call" | custom-call | tf_op jit(solution)/shard_map/gather/pallas_call | solution.py:243
  400.8 1.5 constant_dynamic-slice_fusion
  402.3 1.3 collective-permute-start
  403.6 0.0 copy-start
  403.6 0.0 copy-start.1
  403.7 33.5 %settle.1 = (bf16[5120,1280]{1,0:T(8,128)(2,1)}, bf16[5120,1280]{1,0:T(8,128)(2,1)}, bf16[1280,5120]{1,0:T(8,128)(2,1)}, bf16[5120,1280]{1,0:T(8,128)(2,1)}) custom-call(bf16[5120,1280]{1,0:T(8,128)(2,1)} %get-tuple-element.15.refs_0_, bf16[5120,1280]{1,0:T(8,128)(2,1)} %get-tuple-element.16.refs_1_, bf16[1280,5120]{1,0:T(8,128)(2,1)} %get-tuple-element.17.refs_2_, ...), custom_call_target="tpu_custom_call" | custom-call | bytes 104857600 | tf_op jit(solution)/shard_map/settle/pallas_call | solution.py:275
  437.2 5.1 %collective-permute-done.got_ref = bf16[640,1280]{1,0:T(8,128)(2,1)S(1)} collective-permute-done((bf16[640,1280]{1,0:T(8,128)(2,1)S(1)}, bf16[640,1280]{1,0:T(8,128)(2,1)S(1)}, u32[]{:S(2)}, u32[]{:S(2)}) %collective-permute-start) | collective-permute-done | bytes 1638432 | tf_op jit(solution)/shard_map/ppermute | solution.py:266
  442.3 1.9 collective-permute-start.1
  444.2 0.0 copy-done
  444.2 0.0 copy-done.1
  444.3 0.2 dynamic-update-slice
  444.5 38.9 %all-reduce = bf16[5120]{0:T(1024)(128)(2,1)} all-reduce(bf16[5120]{0:T(1024)(128)(2,1)S(1)} %dynamic-update-slice), channel_id=1, replica_groups=mesh['fsdp'=8,'cols'=4] {'fsdp','cols'}, use_global_device_ids=true, to_apply=%add | all-reduce | flops 5120 | bytes 20480
  483.4 0.0 collective-permute-done.1.other_ref
  483.4 2.1 patch.1
  (2 shorter events, 0.0 us)
Async XLA Ops:
  402.3 40.0 %collective-permute-start = (bf16[640,1280]{1,0:T(8,128)(2,1)S(1)}, bf16[640,1280]{1,0:T(8,128)(2,1)S(1)}, u32[]{:S(2)}, u32[]{:S(2)}) collective-permute-start(bf16[640,1280]{1,0:T(8,128)(2,1)S(1)} %constant_dynamic-slice_fusion), channel_id=1, source_target_pairs={{16,24},{20,28},{8,0},{12,4},{17,25},{21,29},{9,1},{13,5},{18,26},... | collective-permute-start | bytes 4915208 | tf_op jit(solution)/shard_map/ppermute | solution.py:266
  403.6 40.6 %copy-start = (f32[160]{0:T(256)S(1)}, f32[160]{0:T(256)}, u32[]{:S(2)}) copy-start(f32[160]{0:T(256)} %param.26) | copy-start | bytes 1924
  403.6 40.6 %copy-start.1 = (f32[160]{0:T(256)S(1)}, f32[160]{0:T(256)}, u32[]{:S(2)}) copy-start(f32[160]{0:T(256)} %param.27) | copy-start | bytes 1924
  442.3 41.1 %collective-permute-start.1 = (bf16[640,1280]{1,0:T(8,128)(2,1)S(1)}, bf16[640,1280]{1,0:T(8,128)(2,1)S(1)}, u32[]{:S(2)}, u32[]{:S(2)}) collective-permute-start(bf16[640,1280]{1,0:T(8,128)(2,1)S(1)} %collective-permute-done.got_ref), channel_id=1, source_target_pairs={{0,4},{4,0},{24,28},{28,24},{1,5},{5,1},{25,29},{29,25},{2,6},{6,2... | collective-permute-start | bytes 4915208 | tf_op jit(solution)/shard_map/ppermute | solution.py:292
